TPU v7x, 512 devices: a whole 4x8x8 slice. The times are simulated.
512 devices in a mesh: ta: 64 (over z, y_lo, x), sa: 8 (over y_hi, core).
Axes of the slice: x: 4, y: 8 (y_hi: 4, y_lo: 2; y = y_hi * 2 + y_lo), z: 8, core: 2. Of those that a mesh axis runs over, the one named last changes fastest.
Arguments:
- rhs: float32 [1, 2, 40, 64, 8, 128], P(None, None, None, 'ta', 'sa'), may hold values from -6 to 6
- links: bfloat16 [4, 2, 40, 40, 64, 8, 128], P(None, None, None, None, 'ta', 'sa'), may hold values from -0.625 to 0.625
- clover: bfloat16 [2, 40, 40, 64, 8, 128], P(None, None, None, 'ta', 'sa'), may hold values from -1 to 7
- mr_steps: int32 [64, 8, 2], P('ta', 'sa'), may hold values from 2 to 3
Outputs:
- solution: float32 [1, 2, 40, 64, 8, 128], P(None, None, None, 'ta', 'sa')
- residual: float32 [1, 2, 40, 64, 8, 128], P(None, None, None, 'ta', 'sa')
All inputs are finite; a program needn't handle non-finite values.
Results may differ from a plain program's by a relative error of at most 0.0003.
Values sent between devices are 32-bit elements; how exact they have to be, the bound alone decides.
A program may use at most 128 MiB of HBM per device.

v0:
```python
import functools

import jax
import jax.numpy as jnp
from jax import lax
from jax.experimental import pallas as pl
from jax.experimental.pallas import tpu as pltpu
from jax.sharding import PartitionSpec as P

MESH = pl.DeviceIdType.MESH
MR_MAX = 3
HALF_SWEEPS = 4
DOF = 40
PAIRS = 20
LANES = 128
HALF = 64
CLOVER, ZDIR, YDIR, XDIR, TDIR = 0, 1, 2, 3, 4
LINK_OF = {TDIR: 0, ZDIR: 1, YDIR: 2, XDIR: 3}


def roll(x, amount):
    return pltpu.roll(x, amount % LANES, axis=1)


def fold_rows(x):
    return x[0:8] + x[8:16] + x[16:24] + x[24:32] + x[32:40]


def kernel(
    time_count,
    space_count,
    rhs_ref,
    links_ref,
    clover_ref,
    steps_ref,
    sol_ref,
    res_ref,
    raw,
    mat_a,
    mat_b,
    mat_s,
    resid,
    solu,
    search,
    corr,
    face,
    bcast,
    fwd_re,
    fwd_im,
    tsend,
    zup_send,
    zdn_send,
    trecv,
    zup_recv,
    zdn_recv,
    load_sem,
    send_sem,
    recv_sem,
):
    f32 = jnp.float32
    tpos = lax.axis_index("ta")
    zpos = lax.axis_index("sa")
    t_up = lax.rem(tpos + 1, time_count)
    t_dn = lax.rem(tpos + time_count - 1, time_count)
    z_up = lax.rem(zpos + 1, space_count)
    z_dn = lax.rem(zpos + space_count - 1, space_count)

    def load(mat):
        source = clover_ref if mat == CLOVER else links_ref.at[LINK_OF[mat]]
        return pltpu.make_async_copy(source, raw.at[mat], load_sem.at[mat])

    for mat in (CLOVER, ZDIR, YDIR, XDIR, TDIR):
        load(mat).start()
    barrier = pltpu.get_barrier_semaphore()
    for target in ((t_up, zpos), (t_dn, zpos), (tpos, z_up), (tpos, z_dn)):
        pl.semaphore_signal(barrier, inc=1, device_id=target, device_id_type=MESH)

    lane = lax.broadcasted_iota(jnp.int32, (DOF, LANES), 1)
    row = lax.broadcasted_iota(jnp.int32, (DOF, LANES), 0)
    low = lane < HALF
    site = lane % HALF
    x_at = site % 4
    y_at = (site // 4) % 4
    z_at = site // 16
    sign = jnp.where(row < DOF // 2, 1.0, -1.0).astype(f32)
    low8 = low[0:8]
    tail_keep = (low8 & (row[0:8] < 4)) | (jnp.logical_not(low8) & (row[0:8] >= 4))

    def pack(mat, half):
        keep = low if False else ((lane // HALF) == half)
        first = half == 0

        def one(i, carry):
            group = i // 8
            lo_row = i + 8 * group
            hi_row = lo_row + 8 - 4 * (group // 2)
            parts = []
            for comp in range(2):
                upper = raw[mat, comp, lo_row].astype(f32)
                lower = raw[mat, comp, hi_row].astype(f32)
                mixed = roll(jnp.where(low, lower, upper), HALF)
                own = jnp.where(first, upper, lower)
                parts.append(jnp.where(keep, own, mixed))
            mat_a[half, mat, i] = parts[0]
            mat_b[half, mat, i] = parts[1]
            mat_s[half, mat, i] = parts[0] + parts[1]
            return carry

        lax.fori_loop(0, PAIRS, one, 0, unroll=2)

    def dup(x, half):
        return jnp.where((lane // HALF) == half, x, roll(x, HALF))

    def split_dup(x):
        turned = roll(x, HALF)
        return jnp.where(low, x, turned), jnp.where(low, turned, x)

    def store_bcast(re, im):
        def packed(v):
            tail = v[32:40]
            return jnp.concatenate(
                [
                    jnp.where(low8, v[0:8], v[8:16]),
                    jnp.where(low8, v[16:24], v[24:32]),
                    jnp.where(low8, tail, pltpu.roll(tail, 4, axis=0)),
                ],
                axis=0,
            )

        wr = packed(re * sign)
        wi = packed(im * sign)
        bcast[0] = wr
        bcast[1] = -(wr + wi)
        bcast[2] = wr - wi

    def combos(re, im):
        return re, im - re, re + im

    def forward(i, mats, vec, fresh):
        k1 = fold_rows(mats[2] * vec[0])
        k2 = fold_rows(mats[0] * vec[1])
        k3 = fold_rows(mats[1] * vec[2])
        if fresh:
            fwd_re[i] = k1 - k3
            fwd_im[i] = k1 + k2
        else:
            fwd_re[i] = fwd_re[i] + (k1 - k3)
            fwd_im[i] = fwd_im[i] + (k1 + k2)

    def get(half, mat, i):
        return mat_a[half, mat, i], mat_b[half, mat, i], mat_s[half, mat, i]

    def forward_only(half, mat, re, im, fresh):
        vec = combos(re, im)

        def one(i, carry):
            forward(i, get(half, mat, i), vec, fresh)
            return carry

        lax.fori_loop(0, PAIRS, one, 0, unroll=4)

    def accumulate(i, mats, acc):
        w1 = bcast[0, pl.ds(i, 1), :]
        w2 = bcast[1, pl.ds(i, 1), :]
        w3 = bcast[2, pl.ds(i, 1), :]
        return acc[0] + mats[2] * w1, acc[1] + mats[0] * w2, acc[2] + mats[1] * w3

    def finish(acc):
        return sign * (acc[0] - acc[2]), -sign * (acc[0] + acc[1])

    zeros3 = (jnp.zeros((DOF, LANES), f32),) * 3

    def both(half, mat, re, im):
        vec = combos(re, im)

        def one(i, acc):
            mats = get(half, mat, i)
            forward(i, mats, vec, False)
            return accumulate(i, mats, acc)

        return finish(lax.fori_loop(0, PAIRS, one, zeros3, unroll=4))

    def backward_only(half, mat):
        def one(i, acc):
            return accumulate(i, get(half, mat, i), acc)

        return finish(lax.fori_loop(0, PAIRS, one, zeros3, unroll=4))

    def gather_forward(ref):
        groups = []
        for start, count in ((0, 8), (8, 8), (16, 4)):
            rows = jnp.sum(ref[start : start + count], axis=1)
            if count == 4:
                rows = jnp.concatenate([rows, rows], axis=0)
            turned = roll(rows, HALF)
            if count == 8:
                groups.append(jnp.where(low8, rows, turned))
                groups.append(jnp.where(low8, turned, rows))
            else:
                groups.append(jnp.where(tail_keep, rows, turned))
        return jnp.concatenate(groups, axis=0)

    def total(x):
        lanes = jnp.broadcast_to(jnp.sum(fold_rows(x), axis=1, keepdims=True), (8, LANES))
        lanes = lanes + pltpu.roll(lanes, 4, axis=0)
        lanes = lanes + pltpu.roll(lanes, 2, axis=0)
        lanes = lanes + pltpu.roll(lanes, 1, axis=0)
        return 0.5 * lanes

    def spread(x):
        return jnp.concatenate([x] * 5, axis=0)

    def mr_step(half, step):
        sr, si = search[0], search[1]
        store_bcast(sr, si)
        forward_only(half, CLOVER, sr, si, True)

        def ahead(v, mat):
            if mat == ZDIR:
                return jnp.where(z_at == 3, 0.0, -roll(v, -16))
            if mat == YDIR:
                return -jnp.where(y_at == 3, roll(v, 12), roll(v, -4))
            return -jnp.where(x_at == 3, roll(v, 3), roll(v, -1))

        zr, zi = both(half, ZDIR, ahead(sr, ZDIR), ahead(si, ZDIR))
        zr, zi = roll(zr, 16), roll(zi, 16)
        yr, yi = both(half, YDIR, ahead(sr, YDIR), ahead(si, YDIR))
        xr, xi = both(half, XDIR, ahead(sr, XDIR), ahead(si, XDIR))

        def behind(z, y, x):
            y = jnp.where(y_at == 0, roll(y, -12), roll(y, 4))
            x = jnp.where(x_at == 0, roll(x, -3), roll(x, 1))
            out = jnp.where(z_at == 0, 0.0, z) + y + x
            return out + roll(out, HALF)

        qr = gather_forward(fwd_re) - behind(zr, yr, xr)
        qi = gather_forward(fwd_im) - behind(zi, yi, xi)
        nr = total(qr * sr + qi * si)
        ni = total(qr * si - qi * sr)
        inv = 1.0 / (total(qr * qr + qi * qi) + 1e-6)
        live = step < steps_ref[half]
        ar = spread(jnp.where(live, nr * inv, 0.0))
        ai = spread(jnp.where(live, ni * inv, 0.0))
        corr[0] = corr[0] + (ar * sr - ai * si)
        corr[1] = corr[1] + (ar * si + ai * sr)
        face[0] = face[0] + (ar * zr - ai * zi)
        face[1] = face[1] + (ar * zi + ai * zr)
        search[0] = sr - (ar * qr - ai * qi)
        search[1] = si - (ar * qi + ai * qr)

    first_half = lax.rem(zpos, 2)
    for comp in range(2):
        full = rhs_ref[comp]
        for half in range(2):
            resid[half, comp] = dup(full, half)
            solu[half, comp] = jnp.zeros((DOF, LANES), f32)

    for mat in (CLOVER, ZDIR, YDIR, XDIR, TDIR):
        load(mat).wait()
        pack(mat, first_half)

    pl.semaphore_wait(barrier, 4)

    def copies(turn, t_to):
        t_copy = pltpu.make_async_remote_copy(
            src_ref=tsend.at[turn],
            dst_ref=trecv.at[turn],
            send_sem=send_sem.at[turn, 0],
            recv_sem=recv_sem.at[turn, 0],
            device_id=(t_to, zpos),
            device_id_type=MESH,
        )
        up_copy = pltpu.make_async_remote_copy(
            src_ref=zup_send.at[turn],
            dst_ref=zup_recv.at[turn],
            send_sem=send_sem.at[turn, 1],
            recv_sem=recv_sem.at[turn, 1],
            device_id=(tpos, z_up),
            device_id_type=MESH,
        )
        dn_copy = pltpu.make_async_remote_copy(
            src_ref=zdn_send.at[turn],
            dst_ref=zdn_recv.at[turn],
            send_sem=send_sem.at[turn, 2],
            recv_sem=recv_sem.at[turn, 2],
            device_id=(tpos, z_dn),
            device_id_type=MESH,
        )
        return t_copy, up_copy, dn_copy

    def half_sweep(turn, carry):
        half = lax.rem(turn + zpos, 2)
        other = 1 - half
        t_to = jnp.where(half == 0, t_dn, t_up)
        t_copy, up_copy, dn_copy = copies(turn, t_to)
        for comp in range(2):
            search[comp] = resid[half, comp]
            corr[comp] = jnp.zeros((DOF, LANES), f32)
            face[comp] = jnp.zeros((DOF, LANES), f32)

        def step(k, c):
            mr_step(half, k)
            return c

        lax.fori_loop(0, MR_MAX, step, 0)
        er, ei = corr[0], corr[1]
        zdn_send[turn] = roll(jnp.where(low, ei, er), -16)
        dn_copy.start()
        fr, fi = face[0], face[1]
        fr = fr + roll(fr, HALF)
        fi = fi + roll(fi, HALF)
        zup_send[turn] = jnp.where(low, fr, fi)
        up_copy.start()
        store_bcast(er, ei)

        @pl.when(half == 0)
        def _():
            tsend[turn] = jnp.where(low, er, ei)
            t_copy.start()

        pr, pi = backward_only(half, TDIR)
        pr = pr + roll(pr, HALF)
        pi = pi + roll(pi, HALF)

        @pl.when(half == 1)
        def _():
            tsend[turn] = jnp.where(low, pr, pi)
            t_copy.start()

        for comp in range(2):
            resid[half, comp] = search[comp]
            solu[half, comp] = solu[half, comp] + corr[comp]
        face[0] = pr
        face[1] = pi

        @pl.when(turn == 0)
        def _():
            for mat in (TDIR, ZDIR, CLOVER, YDIR, XDIR):
                pack(mat, other)

        @pl.when(half == 1)
        def _():
            forward_only(other, TDIR, corr[0], corr[1], True)

        t_copy.wait_recv()

        @pl.when(half == 0)
        def _():
            tr, ti = split_dup(trecv[turn])
            forward_only(other, TDIR, tr, ti, True)

        @pl.when(half == 1)
        def _():
            tr, ti = split_dup(trecv[turn])
            face[0] = tr
            face[1] = ti

        dn_copy.wait_recv()
        zr, zi = split_dup(zdn_recv[turn])
        forward_only(
            other,
            ZDIR,
            jnp.where(z_at == 3, zr, 0.0),
            jnp.where(z_at == 3, zi, 0.0),
            False,
        )
        up_copy.wait_recv()
        ur, ui = split_dup(zup_recv[turn])
        ur = jnp.where(z_at == 0, ur, 0.0)
        ui = jnp.where(z_at == 0, ui, 0.0)
        resid[other, 0] = resid[other, 0] + gather_forward(fwd_re) + face[0] + ur
        resid[other, 1] = resid[other, 1] + gather_forward(fwd_im) + face[1] + ui
        return carry

    lax.fori_loop(0, HALF_SWEEPS, half_sweep, 0)

    for comp in range(2):
        sol_ref[comp] = jnp.where(low, solu[0, comp], solu[1, comp])
        res_ref[comp] = jnp.where(low, resid[0, comp], resid[1, comp])

    def drain(turn, carry):
        for copy in copies(turn, t_up):
            copy.wait_send()
        return carry

    lax.fori_loop(0, HALF_SWEEPS, drain, 0)


def solution(mesh):
    time_count, space_count = mesh.shape["ta"], mesh.shape["sa"]
    f32 = jnp.float32
    vmem = pltpu.VMEM
    field = (2, DOF, LANES)

    def shards(rhs, links, clover, mr_steps):
        out = jax.ShapeDtypeStruct(field, f32)
        packed = vmem((2, 5, PAIRS, DOF, LANES), f32)
        message = vmem((HALF_SWEEPS, DOF, LANES), f32)
        sol, res = pl.pallas_call(
            functools.partial(kernel, time_count, space_count),
            out_shape=(out, out),
            in_specs=[
                pl.BlockSpec(memory_space=pltpu.VMEM),
                pl.BlockSpec(memory_space=pl.ANY),
                pl.BlockSpec(memory_space=pl.ANY),
                pl.BlockSpec(memory_space=pltpu.SMEM),
            ],
            out_specs=(pl.BlockSpec(memory_space=pltpu.VMEM),) * 2,
            scratch_shapes=[
                vmem((5, 2, DOF, DOF, LANES), jnp.bfloat16),
                packed,
                packed,
                packed,
                vmem((2,) + field, f32),
                vmem((2,) + field, f32),
                vmem(field, f32),
                vmem(field, f32),
                vmem(field, f32),
                vmem((3, 24, LANES), f32),
                vmem((PAIRS, 8, LANES), f32),
                vmem((PAIRS, 8, LANES), f32),
                message,
                message,
                message,
                message,
                message,
                message,
                pltpu.SemaphoreType.DMA((5,)),
                pltpu.SemaphoreType.DMA((HALF_SWEEPS, 3)),
                pltpu.SemaphoreType.DMA((HALF_SWEEPS, 3)),
            ],
            compiler_params=pltpu.CompilerParams(
                collective_id=0, has_side_effects=True, vmem_limit_bytes=50 * 2**20
            ),
        )(
            rhs.reshape(field),
            links.reshape(4, 2, DOF, DOF, LANES),
            clover.reshape(2, DOF, DOF, LANES),
            mr_steps.reshape(2),
        )
        shape = rhs.shape
        return sol.reshape(shape), res.reshape(shape)

    placed = (
        P(None, None, None, "ta", "sa", None),
        P(None, None, None, None, "ta", "sa", None),
        P(None, None, None, "ta", "sa", None),
        P("ta", "sa", None),
    )
    return jax.shard_map(
        shards,
        mesh=mesh,
        in_specs=placed,
        out_specs=(P(None, None, None, "ta", "sa", None),) * 2,
        check_vma=False,
    )
```

profile of v0, /device:TPU:16, one launch (start us, length us, event | category | flops | bytes accessed | tf_op | source)
XLA Modules:
  0.0 58.0 jit_solution(16432158946147621609)
XLA Ops:
  0.6 0.0 copy-start
  0.6 1.1 %copy-done = bf16[2,40,40,1,1,128]{5,2,4,3,1,0:T(8,128)(2,1)S(1)} copy-done((bf16[2,40,40,1,1,128]{5,2,4,3,1,0:T(8,128)(2,1)S(1)}, bf16[2,40,40,1,1,128]{5,2,4,3,1,0:T(8,128)(2,1)}, u32[]{:S(2)}) %copy-start) | copy-done | bytes 819224
  1.8 0.0 copy-start.1
  1.8 0.8 %copy-done.1 = f32[1,2,40,1,1,128]{5,4,3,2,1,0:T(1,128)S(1)} copy-done((f32[1,2,40,1,1,128]{5,4,3,2,1,0:T(1,128)S(1)}, f32[1,2,40,1,1,128]{5,4,3,2,1,0:T(1,128)}, u32[]{:S(2)}) %copy-start.1) | copy-done | bytes 40984
  2.6 0.0 copy-start.2
  2.6 0.7 %copy-done.2 = s32[1,1,2]{2,1,0:T(1,128)S(1)} copy-done((s32[1,1,2]{2,1,0:T(1,128)S(1)}, s32[1,1,2]{2,1,0:T(1,128)}, u32[]{:S(2)}) %copy-start.2) | copy-done | bytes 32
  3.2 53.5 %shard_map.59 = (f32[2,40,128]{2,1,0:T(8,128)S(1)}, f32[2,40,128]{2,1,0:T(8,128)S(1)}) custom-call(f32[2,40,128]{2,1,0:T(8,128)S(1)} %bitcast.11, bf16[4,2,40,40,128]{4,3,2,1,0:T(8,128)(2,1)} %bitcast.15, bf16[2,40,40,128]{3,2,1,0:T(8,128)(2,1)S(1)} %bitcast.10, s32[2]{0:T(128)S(1)} %bitcast.14), custom_call_target="tpu_custom_call" | custom-call | tf_op jit(solution)/shard_map/pallas_call | solution.py:399
  56.7 0.6 %copy.10 = f32[1,2,40,1,1,128]{5,4,3,2,1,0:T(1,128)} copy(f32[1,2,40,1,1,128]{5,4,3,2,1,0:T(1,128)S(1)} %bitcast.13) | data formatting | bytes 81920
  57.3 0.6 %copy.11 = f32[1,2,40,1,1,128]{5,4,3,2,1,0:T(1,128)} copy(f32[1,2,40,1,1,128]{5,4,3,2,1,0:T(1,128)S(1)} %bitcast.12) | data formatting | bytes 81920
Async XLA Ops:
  0.6 1.1 %copy-start = (bf16[2,40,40,1,1,128]{5,2,4,3,1,0:T(8,128)(2,1)S(1)}, bf16[2,40,40,1,1,128]{5,2,4,3,1,0:T(8,128)(2,1)}, u32[]{:S(2)}) copy-start(bf16[2,40,40,1,1,128]{5,2,4,3,1,0:T(8,128)(2,1)} %param.6) | copy-start | bytes 2457604
  1.8 0.8 %copy-start.1 = (f32[1,2,40,1,1,128]{5,4,3,2,1,0:T(1,128)S(1)}, f32[1,2,40,1,1,128]{5,4,3,2,1,0:T(1,128)}, u32[]{:S(2)}) copy-start(f32[1,2,40,1,1,128]{5,4,3,2,1,0:T(1,128)} %param.4) | copy-start | bytes 122884
  2.6 0.7 %copy-start.2 = (s32[1,1,2]{2,1,0:T(1,128)S(1)}, s32[1,1,2]{2,1,0:T(1,128)}, u32[]{:S(2)}) copy-start(s32[1,1,2]{2,1,0:T(1,128)} %param.7) | copy-start | bytes 28
where the time goes:
time: 58.2 us; the launch traced here: 58 us
  Pallas kernels  53.5 us (92%)
  local copies, waits for them, and re-layouts  3.81 us (7%)
  between operations  0.65 us (1%)
    pallas_call x1, Pallas kernels, shards(): pl.pallas_call(functools.partial(kernel, time_count, space_count), out_sh...  53.5 us
    unnamed x8, local copies, waits for them, and re-layouts  3.81 us

commit v1 on v0

--- a/solution.py
+++ b/solution.py
@@ -29,21 +29,17 @@
 def kernel(
     time_count,
     space_count,
-    rhs_ref,
+    rhs_hbm,
     links_ref,
     clover_ref,
     steps_ref,
     sol_ref,
     res_ref,
+    mats,
     raw,
-    mat_a,
-    mat_b,
-    mat_s,
     resid,
     solu,
-    search,
-    corr,
-    face,
+    state,
     bcast,
     fwd_re,
     fwd_im,
@@ -58,6 +54,7 @@
     recv_sem,
 ):
     f32 = jnp.float32
+    search, corr, face, rhs_ref = (state.at[pl.ds(2 * k, 2)] for k in range(4))
     tpos = lax.axis_index("ta")
     zpos = lax.axis_index("sa")
     t_up = lax.rem(tpos + 1, time_count)
@@ -69,6 +66,8 @@
         source = clover_ref if mat == CLOVER else links_ref.at[LINK_OF[mat]]
         return pltpu.make_async_copy(source, raw.at[mat], load_sem.at[mat])
 
+    rhs_load = pltpu.make_async_copy(rhs_hbm, rhs_ref, load_sem.at[5])
+    rhs_load.start()
     for mat in (CLOVER, ZDIR, YDIR, XDIR, TDIR):
         load(mat).start()
     barrier = pltpu.get_barrier_semaphore()
@@ -87,26 +86,21 @@
     tail_keep = (low8 & (row[0:8] < 4)) | (jnp.logical_not(low8) & (row[0:8] >= 4))
 
     def pack(mat, half):
-        keep = low if False else ((lane // HALF) == half)
-        first = half == 0
-
-        def one(i, carry):
-            group = i // 8
-            lo_row = i + 8 * group
-            hi_row = lo_row + 8 - 4 * (group // 2)
+        source = lax.broadcasted_iota(jnp.int32, (2 * LANES, LANES), 0)
+        target = lax.broadcasted_iota(jnp.int32, (2 * LANES, LANES), 1)
+        wanted = (target // HALF) * LANES + half * HALF + target % HALF
+        select = jnp.where(source == wanted, 1.0, 0.0).astype(jnp.bfloat16)
+        for out_at, lo_at, hi_at, count in ((0, 0, 8, 8), (8, 16, 24, 8), (16, 32, 36, 4)):
             parts = []
             for comp in range(2):
-                upper = raw[mat, comp, lo_row].astype(f32)
-                lower = raw[mat, comp, hi_row].astype(f32)
-                mixed = roll(jnp.where(low, lower, upper), HALF)
-                own = jnp.where(first, upper, lower)
-                parts.append(jnp.where(keep, own, mixed))
-            mat_a[half, mat, i] = parts[0]
-            mat_b[half, mat, i] = parts[1]
-            mat_s[half, mat, i] = parts[0] + parts[1]
-            return carry
-
-        lax.fori_loop(0, PAIRS, one, 0, unroll=2)
+                upper = raw[mat, comp, lo_at : lo_at + count].reshape(count * DOF, LANES)
+                lower = raw[mat, comp, hi_at : hi_at + count].reshape(count * DOF, LANES)
+                both_rows = jnp.concatenate([upper, lower], axis=1)
+                out = jnp.dot(both_rows, select, preferred_element_type=f32)
+                parts.append(out.reshape(count, DOF, LANES))
+            mats[half, mat, out_at : out_at + count, 0] = parts[0]
+            mats[half, mat, out_at : out_at + count, 1] = parts[1]
+            mats[half, mat, out_at : out_at + count, 2] = parts[0] + parts[1]
 
     def dup(x, half):
         return jnp.where((lane // HALF) == half, x, roll(x, HALF))
@@ -129,17 +123,17 @@
 
         wr = packed(re * sign)
         wi = packed(im * sign)
-        bcast[0] = wr
-        bcast[1] = -(wr + wi)
-        bcast[2] = wr - wi
+        bcast[0, 0:24] = wr
+        bcast[1, 0:24] = -(wr + wi)
+        bcast[2, 0:24] = wr - wi
 
     def combos(re, im):
         return re, im - re, re + im
 
-    def forward(i, mats, vec, fresh):
-        k1 = fold_rows(mats[2] * vec[0])
-        k2 = fold_rows(mats[0] * vec[1])
-        k3 = fold_rows(mats[1] * vec[2])
+    def forward(i, block, vec, fresh):
+        k1 = fold_rows(block[2] * vec[0])
+        k2 = fold_rows(block[0] * vec[1])
+        k3 = fold_rows(block[1] * vec[2])
         if fresh:
             fwd_re[i] = k1 - k3
             fwd_im[i] = k1 + k2
@@ -148,7 +142,7 @@
             fwd_im[i] = fwd_im[i] + (k1 + k2)
 
     def get(half, mat, i):
-        return mat_a[half, mat, i], mat_b[half, mat, i], mat_s[half, mat, i]
+        return tuple(mats[half, mat, i, k] for k in range(3))
 
     def forward_only(half, mat, re, im, fresh):
         vec = combos(re, im)
@@ -157,13 +151,13 @@
             forward(i, get(half, mat, i), vec, fresh)
             return carry
 
-        lax.fori_loop(0, PAIRS, one, 0, unroll=4)
-
-    def accumulate(i, mats, acc):
+        lax.fori_loop(0, PAIRS, one, 0, unroll=20)
+
+    def accumulate(i, block, acc):
         w1 = bcast[0, pl.ds(i, 1), :]
         w2 = bcast[1, pl.ds(i, 1), :]
         w3 = bcast[2, pl.ds(i, 1), :]
-        return acc[0] + mats[2] * w1, acc[1] + mats[0] * w2, acc[2] + mats[1] * w3
+        return acc[0] + block[2] * w1, acc[1] + block[0] * w2, acc[2] + block[1] * w3
 
     def finish(acc):
         return sign * (acc[0] - acc[2]), -sign * (acc[0] + acc[1])
@@ -174,26 +168,38 @@
         vec = combos(re, im)
 
         def one(i, acc):
-            mats = get(half, mat, i)
-            forward(i, mats, vec, False)
-            return accumulate(i, mats, acc)
-
-        return finish(lax.fori_loop(0, PAIRS, one, zeros3, unroll=4))
+            block = get(half, mat, i)
+            forward(i, block, vec, False)
+            return accumulate(i, block, acc)
+
+        return finish(lax.fori_loop(0, PAIRS, one, zeros3, unroll=20))
 
     def backward_only(half, mat):
         def one(i, acc):
             return accumulate(i, get(half, mat, i), acc)
 
-        return finish(lax.fori_loop(0, PAIRS, one, zeros3, unroll=4))
+        return finish(lax.fori_loop(0, PAIRS, one, zeros3, unroll=20))
+
+    sub = lax.broadcasted_iota(jnp.int32, (8, LANES), 0)
+
+    def pair(lo, hi, width):
+        keep = (sub & width) == 0
+        return jnp.where(keep, lo, hi) + pltpu.roll(jnp.where(keep, hi, lo), width, axis=0)
+
+    def fold_eight(tiles):
+        ones = [pair(tiles[2 * k], tiles[2 * k + 1], 1) for k in range(4)]
+        twos = [pair(ones[2 * k], ones[2 * k + 1], 2) for k in range(2)]
+        return pair(twos[0], twos[1], 4)
 
     def gather_forward(ref):
         groups = []
-        for start, count in ((0, 8), (8, 8), (16, 4)):
-            rows = jnp.sum(ref[start : start + count], axis=1)
-            if count == 4:
-                rows = jnp.concatenate([rows, rows], axis=0)
+        for start in (0, 8, 16):
+            if start < 16:
+                rows = fold_eight([ref[start + k] for k in range(8)])
+            else:
+                rows = fold_eight([ref[start + k % 4] for k in range(8)])
             turned = roll(rows, HALF)
-            if count == 8:
+            if start < 16:
                 groups.append(jnp.where(low8, rows, turned))
                 groups.append(jnp.where(low8, turned, rows))
             else:
@@ -249,6 +255,7 @@
         search[1] = si - (ar * qi + ai * qr)
 
     first_half = lax.rem(zpos, 2)
+    rhs_load.wait()
     for comp in range(2):
         full = rhs_ref[comp]
         for half in range(2):
@@ -258,8 +265,6 @@
     for mat in (CLOVER, ZDIR, YDIR, XDIR, TDIR):
         load(mat).wait()
         pack(mat, first_half)
-
-    pl.semaphore_wait(barrier, 4)
 
     def copies(turn, t_to):
         t_copy = pltpu.make_async_remote_copy(
@@ -303,21 +308,26 @@
             return c
 
         lax.fori_loop(0, MR_MAX, step, 0)
+
+        @pl.when(turn == 0)
+        def _():
+            pl.semaphore_wait(barrier, 4)
+
         er, ei = corr[0], corr[1]
+
+        @pl.when(half == 0)
+        def _():
+            tsend[turn] = jnp.where(low, er, ei)
+            t_copy.start()
+
         zdn_send[turn] = roll(jnp.where(low, ei, er), -16)
-        dn_copy.start()
         fr, fi = face[0], face[1]
         fr = fr + roll(fr, HALF)
         fi = fi + roll(fi, HALF)
         zup_send[turn] = jnp.where(low, fr, fi)
+        dn_copy.start()
         up_copy.start()
         store_bcast(er, ei)
-
-        @pl.when(half == 0)
-        def _():
-            tsend[turn] = jnp.where(low, er, ei)
-            t_copy.start()
-
         pr, pi = backward_only(half, TDIR)
         pr = pr + roll(pr, HALF)
         pi = pi + roll(pi, HALF)
@@ -337,23 +347,6 @@
         def _():
             for mat in (TDIR, ZDIR, CLOVER, YDIR, XDIR):
                 pack(mat, other)
-
-        @pl.when(half == 1)
-        def _():
-            forward_only(other, TDIR, corr[0], corr[1], True)
-
-        t_copy.wait_recv()
-
-        @pl.when(half == 0)
-        def _():
-            tr, ti = split_dup(trecv[turn])
-            forward_only(other, TDIR, tr, ti, True)
-
-        @pl.when(half == 1)
-        def _():
-            tr, ti = split_dup(trecv[turn])
-            face[0] = tr
-            face[1] = ti
 
         dn_copy.wait_recv()
         zr, zi = split_dup(zdn_recv[turn])
@@ -362,14 +355,42 @@
             ZDIR,
             jnp.where(z_at == 3, zr, 0.0),
             jnp.where(z_at == 3, zi, 0.0),
-            False,
+            True,
         )
+
+        @pl.when(half == 1)
+        def _():
+            forward_only(other, TDIR, corr[0], corr[1], False)
+
         up_copy.wait_recv()
         ur, ui = split_dup(zup_recv[turn])
-        ur = jnp.where(z_at == 0, ur, 0.0)
-        ui = jnp.where(z_at == 0, ui, 0.0)
-        resid[other, 0] = resid[other, 0] + gather_forward(fwd_re) + face[0] + ur
-        resid[other, 1] = resid[other, 1] + gather_forward(fwd_im) + face[1] + ui
+        ur = jnp.where(z_at == 0, ur, 0.0) + resid[other, 0]
+        ui = jnp.where(z_at == 0, ui, 0.0) + resid[other, 1]
+
+        @pl.when(half == 1)
+        def _():
+            resid[other, 0] = ur + gather_forward(fwd_re)
+            resid[other, 1] = ui + gather_forward(fwd_im)
+
+        @pl.when(half == 0)
+        def _():
+            resid[other, 0] = ur + face[0]
+            resid[other, 1] = ui + face[1]
+
+        t_copy.wait_recv()
+        tr, ti = split_dup(trecv[turn])
+
+        @pl.when(half == 0)
+        def _():
+            forward_only(other, TDIR, tr, ti, False)
+            resid[other, 0] = resid[other, 0] + gather_forward(fwd_re)
+            resid[other, 1] = resid[other, 1] + gather_forward(fwd_im)
+
+        @pl.when(half == 1)
+        def _():
+            resid[other, 0] = resid[other, 0] + tr
+            resid[other, 1] = resid[other, 1] + ti
+
         return carry
 
     lax.fori_loop(0, HALF_SWEEPS, half_sweep, 0)
@@ -394,29 +415,24 @@
 
     def shards(rhs, links, clover, mr_steps):
         out = jax.ShapeDtypeStruct(field, f32)
-        packed = vmem((2, 5, PAIRS, DOF, LANES), f32)
         message = vmem((HALF_SWEEPS, DOF, LANES), f32)
         sol, res = pl.pallas_call(
             functools.partial(kernel, time_count, space_count),
             out_shape=(out, out),
             in_specs=[
-                pl.BlockSpec(memory_space=pltpu.VMEM),
-                pl.BlockSpec(memory_space=pl.ANY),
-                pl.BlockSpec(memory_space=pl.ANY),
+                pl.BlockSpec(memory_space=pltpu.HBM),
+                pl.BlockSpec(memory_space=pltpu.HBM),
+                pl.BlockSpec(memory_space=pltpu.HBM),
                 pl.BlockSpec(memory_space=pltpu.SMEM),
             ],
             out_specs=(pl.BlockSpec(memory_space=pltpu.VMEM),) * 2,
             scratch_shapes=[
+                vmem((2, 5, PAIRS, 3, DOF, LANES), f32),
                 vmem((5, 2, DOF, DOF, LANES), jnp.bfloat16),
-                packed,
-                packed,
-                packed,
                 vmem((2,) + field, f32),
                 vmem((2,) + field, f32),
-                vmem(field, f32),
-                vmem(field, f32),
-                vmem(field, f32),
-                vmem((3, 24, LANES), f32),
+                vmem((8, DOF, LANES), f32),
+                vmem((3, 32, LANES), f32),
                 vmem((PAIRS, 8, LANES), f32),
                 vmem((PAIRS, 8, LANES), f32),
                 message,
@@ -425,12 +441,12 @@
                 message,
                 message,
                 message,
-                pltpu.SemaphoreType.DMA((5,)),
+                pltpu.SemaphoreType.DMA((6,)),
                 pltpu.SemaphoreType.DMA((HALF_SWEEPS, 3)),
                 pltpu.SemaphoreType.DMA((HALF_SWEEPS, 3)),
             ],
             compiler_params=pltpu.CompilerParams(
-                collective_id=0, has_side_effects=True, vmem_limit_bytes=50 * 2**20
+                collective_id=0, has_side_effects=True, vmem_limit_bytes=67043328
             ),
         )(
             rhs.reshape(field),

time: 58.2 us -> 47.2 us (0.81)
  Pallas kernels: 53.5 us -> 43.5 us
  local copies, waits for them, and re-layouts: 3.81 us -> 2.8 us
    pallas_call x1, Pallas kernels: 53.5 us -> 43.5 us  [shards(): pl.pallas_call(functools.partial(kernel, time_count, space_count), out_sh...]
    unnamed x8 -> x2, local copies, waits for them, and re-layouts: 3.81 us -> 2.8 us
where the time goes in v1:
time: 47.2 us; the launch traced here: 46.9 us
  Pallas kernels  43.5 us (92%)
  local copies, waits for them, and re-layouts  2.8 us (6%)
  between operations  0.64 us (1%)
    pallas_call x1, Pallas kernels, shards(): pl.pallas_call(functools.partial(kernel, time_count, space_count), out_sh...  43.5 us
    unnamed x2, local copies, waits for them, and re-layouts  2.8 us

profile of v1, /device:TPU:16, one launch (start us, length us, event | category | flops | bytes accessed | tf_op | source)
XLA Modules:
  0.0 46.9 jit_solution(11550145275134902224)
XLA Ops:
  0.6 43.5 %shard_map.59 = (f32[2,40,128]{2,1,0:T(8,128)}, f32[2,40,128]{2,1,0:T(8,128)}) custom-call(f32[2,40,128]{2,1,0:T(8,128)} %bitcast.12, bf16[4,2,40,40,128]{4,3,2,1,0:T(8,128)(2,1)} %bitcast.10, bf16[2,40,40,128]{3,2,1,0:T(8,128)(2,1)} %bitcast.11, s32[2]{0:T(128)} %bitcast.15), custom_call_target="tpu_custom_call" | custom-call | tf_op jit(solution)/shard_map/pallas_call | solution.py:419
  44.1 1.4 %copy.10 = f32[1,2,40,1,1,128]{5,4,3,2,1,0:T(1,128)} copy(f32[1,2,40,1,1,128]{5,4,3,2,1,0:T(1,128)} %bitcast.14) | data formatting | bytes 81920
  45.5 1.4 %copy.11 = f32[1,2,40,1,1,128]{5,4,3,2,1,0:T(1,128)} copy(f32[1,2,40,1,1,128]{5,4,3,2,1,0:T(1,128)} %bitcast.13) | data formatting | bytes 81920

commit v2 on v1

--- a/solution.py
+++ b/solution.py
@@ -32,7 +32,7 @@
     rhs_hbm,
     links_ref,
     clover_ref,
-    steps_ref,
+    steps_hbm,
     sol_ref,
     res_ref,
     mats,
@@ -49,6 +49,7 @@
     trecv,
     zup_recv,
     zdn_recv,
+    steps_ref,
     load_sem,
     send_sem,
     recv_sem,
@@ -68,6 +69,8 @@
 
     rhs_load = pltpu.make_async_copy(rhs_hbm, rhs_ref, load_sem.at[5])
     rhs_load.start()
+    steps_load = pltpu.make_async_copy(steps_hbm, steps_ref, load_sem.at[6])
+    steps_load.start()
     for mat in (CLOVER, ZDIR, YDIR, XDIR, TDIR):
         load(mat).start()
     barrier = pltpu.get_barrier_semaphore()
@@ -109,6 +112,25 @@
         turned = roll(x, HALF)
         return jnp.where(low, x, turned), jnp.where(low, turned, x)
 
+    z8 = z_at[0:8]
+
+    def face_pack(v):
+        tiles = [v[8 * k : 8 * k + 8] for k in range(5)]
+        mixed = tiles[0]
+        for k in range(1, 4):
+            mixed = jnp.where(z8 == k, roll(tiles[k], 16 * k), mixed)
+        return jnp.concatenate([mixed, tiles[4]], axis=0)
+
+    def face_unpack(m, slot):
+        parts = []
+        for k in range(5):
+            tile = m[0:8] if k < 4 else m[8:16]
+            turn = 16 * (slot - k % 4)
+            parts.append((roll(tile, turn), roll(tile, turn + HALF)))
+        re = jnp.concatenate([jnp.where(low8, p, q) for p, q in parts], axis=0)
+        im = jnp.concatenate([jnp.where(low8, q, p) for p, q in parts], axis=0)
+        return jnp.where(z_at == slot, re, 0.0), jnp.where(z_at == slot, im, 0.0)
+
     def store_bcast(re, im):
         def packed(v):
             tail = v[32:40]
@@ -256,6 +278,7 @@
 
     first_half = lax.rem(zpos, 2)
     rhs_load.wait()
+    steps_load.wait()
     for comp in range(2):
         full = rhs_ref[comp]
         for half in range(2):
@@ -320,11 +343,11 @@
             tsend[turn] = jnp.where(low, er, ei)
             t_copy.start()
 
-        zdn_send[turn] = roll(jnp.where(low, ei, er), -16)
+        zdn_send[turn] = face_pack(jnp.where(low, er, ei))
         fr, fi = face[0], face[1]
         fr = fr + roll(fr, HALF)
         fi = fi + roll(fi, HALF)
-        zup_send[turn] = jnp.where(low, fr, fi)
+        zup_send[turn] = face_pack(jnp.where(low, fr, fi))
         dn_copy.start()
         up_copy.start()
         store_bcast(er, ei)
@@ -349,23 +372,17 @@
                 pack(mat, other)
 
         dn_copy.wait_recv()
-        zr, zi = split_dup(zdn_recv[turn])
-        forward_only(
-            other,
-            ZDIR,
-            jnp.where(z_at == 3, zr, 0.0),
-            jnp.where(z_at == 3, zi, 0.0),
-            True,
-        )
+        zr, zi = face_unpack(zdn_recv[turn], 3)
+        forward_only(other, ZDIR, zr, zi, True)
 
         @pl.when(half == 1)
         def _():
             forward_only(other, TDIR, corr[0], corr[1], False)
 
         up_copy.wait_recv()
-        ur, ui = split_dup(zup_recv[turn])
-        ur = jnp.where(z_at == 0, ur, 0.0) + resid[other, 0]
-        ui = jnp.where(z_at == 0, ui, 0.0) + resid[other, 1]
+        ur, ui = face_unpack(zup_recv[turn], 0)
+        ur = ur + resid[other, 0]
+        ui = ui + resid[other, 1]
 
         @pl.when(half == 1)
         def _():
@@ -416,6 +433,7 @@
     def shards(rhs, links, clover, mr_steps):
         out = jax.ShapeDtypeStruct(field, f32)
         message = vmem((HALF_SWEEPS, DOF, LANES), f32)
+        small = vmem((HALF_SWEEPS, 16, LANES), f32)
         sol, res = pl.pallas_call(
             functools.partial(kernel, time_count, space_count),
             out_shape=(out, out),
@@ -423,7 +441,7 @@
                 pl.BlockSpec(memory_space=pltpu.HBM),
                 pl.BlockSpec(memory_space=pltpu.HBM),
                 pl.BlockSpec(memory_space=pltpu.HBM),
-                pl.BlockSpec(memory_space=pltpu.SMEM),
+                pl.BlockSpec(memory_space=pltpu.HBM),
             ],
             out_specs=(pl.BlockSpec(memory_space=pltpu.VMEM),) * 2,
             scratch_shapes=[
@@ -436,23 +454,24 @@
                 vmem((PAIRS, 8, LANES), f32),
                 vmem((PAIRS, 8, LANES), f32),
                 message,
+                small,
+                small,
                 message,
-                message,
-                message,
-                message,
-                message,
-                pltpu.SemaphoreType.DMA((6,)),
+                small,
+                small,
+                pltpu.SMEM((2,), jnp.int32),
+                pltpu.SemaphoreType.DMA((7,)),
                 pltpu.SemaphoreType.DMA((HALF_SWEEPS, 3)),
                 pltpu.SemaphoreType.DMA((HALF_SWEEPS, 3)),
             ],
             compiler_params=pltpu.CompilerParams(
-                collective_id=0, has_side_effects=True, vmem_limit_bytes=67043328
+                collective_id=0, has_side_effects=True, vmem_limit_bytes=40 * 2**20
             ),
         )(
-            rhs.reshape(field),
-            links.reshape(4, 2, DOF, DOF, LANES),
-            clover.reshape(2, DOF, DOF, LANES),
-            mr_steps.reshape(2),
+            pltpu.with_memory_space_constraint(rhs.reshape(field), pltpu.HBM),
+            pltpu.with_memory_space_constraint(links.reshape(4, 2, DOF, DOF, LANES), pltpu.HBM),
+            pltpu.with_memory_space_constraint(clover.reshape(2, DOF, DOF, LANES), pltpu.HBM),
+            pltpu.with_memory_space_constraint(mr_steps.reshape(2), pltpu.HBM),
         )
         shape = rhs.shape
         return sol.reshape(shape), res.reshape(shape)

time: 47.2 us -> 44 us (0.932)
  local copies, waits for them, and re-layouts: 2.8 us -> 1.24 us
  Pallas kernels: 43.5 us -> 42 us
    unnamed x2, local copies, waits for them, and re-layouts: 2.8 us -> 1.24 us
    pallas_call x1, Pallas kernels: 43.5 us -> 42 us  [shards(): pl.pallas_call(functools.partial(kernel, time_count, space_count), out_sh...]
where the time goes in v2:
time: 44 us; the launch traced here: 43.9 us
  Pallas kernels  42 us (95%)
  local copies, waits for them, and re-layouts  1.24 us (3%)
  between operations  0.64 us (1%)
    pallas_call x1, Pallas kernels, shards(): pl.pallas_call(functools.partial(kernel, time_count, space_count), out_sh...  42 us
    unnamed x2, local copies, waits for them, and re-layouts  1.24 us

profile of v2, /device:TPU:16, one launch (start us, length us, event | category | flops | bytes accessed | tf_op | source)
XLA Modules:
  0.0 43.9 jit_solution(12497485466247966862)
XLA Ops:
  0.6 42.0 %shard_map.59 = (f32[2,40,128]{2,1,0:T(8,128)S(1)}, f32[2,40,128]{2,1,0:T(8,128)S(1)}) custom-call(f32[2,40,128]{2,1,0:T(8,128)} %bitcast.14, bf16[4,2,40,40,128]{4,3,2,1,0:T(8,128)(2,1)} %bitcast.12, bf16[2,40,40,128]{3,2,1,0:T(8,128)(2,1)} %bitcast.13, s32[2]{0:T(128)} %bitcast.15), custom_call_target="tpu_custom_call" | custom-call | tf_op jit(solution)/shard_map/pallas_call | solution.py:437
  42.7 0.6 %copy.10 = f32[1,2,40,1,1,128]{5,4,3,2,1,0:T(1,128)} copy(f32[1,2,40,1,1,128]{5,4,3,2,1,0:T(1,128)S(1)} %bitcast.11) | data formatting | bytes 81920
  43.3 0.6 %copy.11 = f32[1,2,40,1,1,128]{5,4,3,2,1,0:T(1,128)} copy(f32[1,2,40,1,1,128]{5,4,3,2,1,0:T(1,128)S(1)} %bitcast.10) | data formatting | bytes 81920

commit v3 on v2

--- a/solution.py
+++ b/solution.py
@@ -49,6 +49,10 @@
     trecv,
     zup_recv,
     zdn_recv,
+    esend,
+    erecv,
+    asend,
+    arecv,
     steps_ref,
     load_sem,
     send_sem,
@@ -267,14 +271,16 @@
         ni = total(qr * si - qi * sr)
         inv = 1.0 / (total(qr * qr + qi * qi) + 1e-6)
         live = step < steps_ref[half]
-        ar = spread(jnp.where(live, nr * inv, 0.0))
-        ai = spread(jnp.where(live, ni * inv, 0.0))
+        ar8 = jnp.where(live, nr * inv, 0.0)
+        ai8 = jnp.where(live, ni * inv, 0.0)
+        ar, ai = spread(ar8), spread(ai8)
         corr[0] = corr[0] + (ar * sr - ai * si)
         corr[1] = corr[1] + (ar * si + ai * sr)
         face[0] = face[0] + (ar * zr - ai * zi)
         face[1] = face[1] + (ar * zi + ai * zr)
         search[0] = sr - (ar * qr - ai * qi)
         search[1] = si - (ar * qi + ai * qr)
+        return ar8, ai8
 
     first_half = lax.rem(zpos, 2)
     rhs_load.wait()
@@ -289,13 +295,13 @@
         load(mat).wait()
         pack(mat, first_half)
 
-    def copies(turn, t_to):
+    def copies(turn):
         t_copy = pltpu.make_async_remote_copy(
             src_ref=tsend.at[turn],
             dst_ref=trecv.at[turn],
             send_sem=send_sem.at[turn, 0],
             recv_sem=recv_sem.at[turn, 0],
-            device_id=(t_to, zpos),
+            device_id=(t_up, zpos),
             device_id_type=MESH,
         )
         up_copy = pltpu.make_async_remote_copy(
@@ -314,13 +320,28 @@
             device_id=(tpos, z_dn),
             device_id_type=MESH,
         )
-        return t_copy, up_copy, dn_copy
+        early_copy = pltpu.make_async_remote_copy(
+            src_ref=esend.at[turn],
+            dst_ref=erecv.at[turn],
+            send_sem=send_sem.at[turn, 3],
+            recv_sem=recv_sem.at[turn, 3],
+            device_id=(t_dn, zpos),
+            device_id_type=MESH,
+        )
+        alpha_copy = pltpu.make_async_remote_copy(
+            src_ref=asend.at[turn],
+            dst_ref=arecv.at[turn],
+            send_sem=send_sem.at[turn, 4],
+            recv_sem=recv_sem.at[turn, 4],
+            device_id=(t_dn, zpos),
+            device_id_type=MESH,
+        )
+        return t_copy, up_copy, dn_copy, early_copy, alpha_copy
 
     def half_sweep(turn, carry):
         half = lax.rem(turn + zpos, 2)
         other = 1 - half
-        t_to = jnp.where(half == 0, t_dn, t_up)
-        t_copy, up_copy, dn_copy = copies(turn, t_to)
+        t_copy, up_copy, dn_copy, early_copy, alpha_copy = copies(turn)
         for comp in range(2):
             search[comp] = resid[half, comp]
             corr[comp] = jnp.zeros((DOF, LANES), f32)
@@ -330,18 +351,25 @@
             mr_step(half, k)
             return c
 
-        lax.fori_loop(0, MR_MAX, step, 0)
+        lax.fori_loop(0, MR_MAX - 1, step, 0, unroll=True)
 
         @pl.when(turn == 0)
         def _():
             pl.semaphore_wait(barrier, 4)
 
+        @pl.when(half == 0)
+        def _():
+            esend[turn, 0] = jnp.where(low, corr[0], corr[1])
+            esend[turn, 1] = jnp.where(low, search[0], search[1])
+            early_copy.start()
+
+        ar8, ai8 = mr_step(half, MR_MAX - 1)
         er, ei = corr[0], corr[1]
 
         @pl.when(half == 0)
         def _():
-            tsend[turn] = jnp.where(low, er, ei)
-            t_copy.start()
+            asend[turn] = jnp.where(sub < 4, ar8, ai8)
+            alpha_copy.start()
 
         zdn_send[turn] = face_pack(jnp.where(low, er, ei))
         fr, fi = face[0], face[1]
@@ -391,20 +419,27 @@
 
         @pl.when(half == 0)
         def _():
-            resid[other, 0] = ur + face[0]
-            resid[other, 1] = ui + face[1]
-
-        t_copy.wait_recv()
-        tr, ti = split_dup(trecv[turn])
-
-        @pl.when(half == 0)
-        def _():
+            early_copy.wait_recv()
+            tr, ti = split_dup(erecv[turn, 0])
             forward_only(other, TDIR, tr, ti, False)
-            resid[other, 0] = resid[other, 0] + gather_forward(fwd_re)
-            resid[other, 1] = resid[other, 1] + gather_forward(fwd_im)
+            br = ur + face[0] + gather_forward(fwd_re)
+            bi = ui + face[1] + gather_forward(fwd_im)
+            tr, ti = split_dup(erecv[turn, 1])
+            forward_only(other, TDIR, tr, ti, True)
+            gr = gather_forward(fwd_re)
+            gi = gather_forward(fwd_im)
+            alpha_copy.wait_recv()
+            got = arecv[turn]
+            swapped = pltpu.roll(got, 4, axis=0)
+            cr = spread(jnp.where(sub < 4, got, swapped))
+            ci = spread(jnp.where(sub < 4, swapped, got))
+            resid[other, 0] = br + (cr * gr - ci * gi)
+            resid[other, 1] = bi + (cr * gi + ci * gr)
 
         @pl.when(half == 1)
         def _():
+            t_copy.wait_recv()
+            tr, ti = split_dup(trecv[turn])
             resid[other, 0] = resid[other, 0] + tr
             resid[other, 1] = resid[other, 1] + ti
 
@@ -417,8 +452,20 @@
         res_ref[comp] = jnp.where(low, resid[0, comp], resid[1, comp])
 
     def drain(turn, carry):
-        for copy in copies(turn, t_up):
-            copy.wait_send()
+        half = lax.rem(turn + zpos, 2)
+        t_copy, up_copy, dn_copy, early_copy, alpha_copy = copies(turn)
+        up_copy.wait_send()
+        dn_copy.wait_send()
+
+        @pl.when(half == 0)
+        def _():
+            early_copy.wait_send()
+            alpha_copy.wait_send()
+
+        @pl.when(half == 1)
+        def _():
+            t_copy.wait_send()
+
         return carry
 
     lax.fori_loop(0, HALF_SWEEPS, drain, 0)
@@ -459,10 +506,14 @@
                 message,
                 small,
                 small,
+                vmem((HALF_SWEEPS, 2, DOF, LANES), f32),
+                vmem((HALF_SWEEPS, 2, DOF, LANES), f32),
+                vmem((HALF_SWEEPS, 8, LANES), f32),
+                vmem((HALF_SWEEPS, 8, LANES), f32),
                 pltpu.SMEM((2,), jnp.int32),
                 pltpu.SemaphoreType.DMA((7,)),
-                pltpu.SemaphoreType.DMA((HALF_SWEEPS, 3)),
-                pltpu.SemaphoreType.DMA((HALF_SWEEPS, 3)),
+                pltpu.SemaphoreType.DMA((HALF_SWEEPS, 5)),
+                pltpu.SemaphoreType.DMA((HALF_SWEEPS, 5)),
             ],
             compiler_params=pltpu.CompilerParams(
                 collective_id=0, has_side_effects=True, vmem_limit_bytes=40 * 2**20

time: 44 us -> 44 us (level)
  no operation moved by 1% of the time
where the time goes in v3:
time: 44 us; the launch traced here: 43.9 us
  Pallas kernels  42 us (95%)
  local copies, waits for them, and re-layouts  1.24 us (3%)
  between operations  0.64 us (1%)
    pallas_call x1, Pallas kernels, shards(): pl.pallas_call(functools.partial(kernel, time_count, space_count), out_sh...  42 us
    unnamed x2, local copies, waits for them, and re-layouts  1.24 us

profile of v3, /device:TPU:16, one launch (start us, length us, event | category | flops | bytes accessed | tf_op | source)
XLA Modules:
  0.0 43.9 jit_solution(4451513547653346956)
XLA Ops:
  0.6 42.0 %shard_map.59 = (f32[2,40,128]{2,1,0:T(8,128)S(1)}, f32[2,40,128]{2,1,0:T(8,128)S(1)}) custom-call(f32[2,40,128]{2,1,0:T(8,128)} %bitcast.14, bf16[4,2,40,40,128]{4,3,2,1,0:T(8,128)(2,1)} %bitcast.12, bf16[2,40,40,128]{3,2,1,0:T(8,128)(2,1)} %bitcast.13, s32[2]{0:T(128)} %bitcast.15), custom_call_target="tpu_custom_call" | custom-call | tf_op jit(solution)/shard_map/pallas_call | solution.py:484
  42.7 0.6 %copy.10 = f32[1,2,40,1,1,128]{5,4,3,2,1,0:T(1,128)} copy(f32[1,2,40,1,1,128]{5,4,3,2,1,0:T(1,128)S(1)} %bitcast.11) | data formatting | bytes 81920
  43.3 0.6 %copy.11 = f32[1,2,40,1,1,128]{5,4,3,2,1,0:T(1,128)} copy(f32[1,2,40,1,1,128]{5,4,3,2,1,0:T(1,128)S(1)} %bitcast.10) | data formatting | bytes 81920

commit v4 on v2

--- a/solution.py
+++ b/solution.py
@@ -88,10 +88,10 @@
     low8 = low[0:8]
     tail_keep = (low8 & (row[0:8] < 4)) | (jnp.logical_not(low8) & (row[0:8] >= 4))
 
-    def pack(mat, half):
-        source = lax.broadcasted_iota(jnp.int32, (2 * LANES, LANES), 0)
-        target = lax.broadcasted_iota(jnp.int32, (2 * LANES, LANES), 1)
-        wanted = (target // HALF) * LANES + half * HALF + target % HALF
+    def pack(mat):
+        source = lax.broadcasted_iota(jnp.int32, (2 * LANES, 2 * LANES), 0)
+        target = lax.broadcasted_iota(jnp.int32, (2 * LANES, 2 * LANES), 1)
+        wanted = (target // HALF % 2) * LANES + target // LANES * HALF + target % HALF
         select = jnp.where(source == wanted, 1.0, 0.0).astype(jnp.bfloat16)
         for out_at, lo_at, hi_at, count in ((0, 0, 8, 8), (8, 16, 24, 8), (16, 32, 36, 4)):
             parts = []
@@ -99,11 +99,12 @@
                 upper = raw[mat, comp, lo_at : lo_at + count].reshape(count * DOF, LANES)
                 lower = raw[mat, comp, hi_at : hi_at + count].reshape(count * DOF, LANES)
                 both_rows = jnp.concatenate([upper, lower], axis=1)
-                out = jnp.dot(both_rows, select, preferred_element_type=f32)
-                parts.append(out.reshape(count, DOF, LANES))
-            mats[half, mat, out_at : out_at + count, 0] = parts[0]
-            mats[half, mat, out_at : out_at + count, 1] = parts[1]
-            mats[half, mat, out_at : out_at + count, 2] = parts[0] + parts[1]
+                parts.append(jnp.dot(both_rows, select, preferred_element_type=f32))
+            for half in range(2):
+                re, im = (p[:, LANES * half : LANES * half + LANES].reshape(count, DOF, LANES) for p in parts)
+                mats[half, mat, out_at : out_at + count, 0] = re
+                mats[half, mat, out_at : out_at + count, 1] = im
+                mats[half, mat, out_at : out_at + count, 2] = re + im
 
     def dup(x, half):
         return jnp.where((lane // HALF) == half, x, roll(x, HALF))
@@ -276,7 +277,6 @@
         search[0] = sr - (ar * qr - ai * qi)
         search[1] = si - (ar * qi + ai * qr)
 
-    first_half = lax.rem(zpos, 2)
     rhs_load.wait()
     steps_load.wait()
     for comp in range(2):
@@ -287,7 +287,7 @@
 
     for mat in (CLOVER, ZDIR, YDIR, XDIR, TDIR):
         load(mat).wait()
-        pack(mat, first_half)
+        pack(mat)
 
     def copies(turn, t_to):
         t_copy = pltpu.make_async_remote_copy(
@@ -330,7 +330,7 @@
             mr_step(half, k)
             return c
 
-        lax.fori_loop(0, MR_MAX, step, 0)
+        lax.fori_loop(0, MR_MAX, step, 0, unroll=True)
 
         @pl.when(turn == 0)
         def _():
@@ -366,11 +366,6 @@
         face[0] = pr
         face[1] = pi
 
-        @pl.when(turn == 0)
-        def _():
-            for mat in (TDIR, ZDIR, CLOVER, YDIR, XDIR):
-                pack(mat, other)
-
         dn_copy.wait_recv()
         zr, zi = face_unpack(zdn_recv[turn], 3)
         forward_only(other, ZDIR, zr, zi, True)
@@ -422,6 +417,15 @@
         return carry
 
     lax.fori_loop(0, HALF_SWEEPS, drain, 0)
+
+
+def write_out(sol_in, res_in, sol_hbm, res_hbm, sems):
+    first = pltpu.make_async_copy(sol_in, sol_hbm, sems.at[0])
+    second = pltpu.make_async_copy(res_in, res_hbm, sems.at[1])
+    first.start()
+    second.start()
+    first.wait()
+    second.wait()
 
 
 def solution(mesh):
@@ -473,6 +477,14 @@
             pltpu.with_memory_space_constraint(clover.reshape(2, DOF, DOF, LANES), pltpu.HBM),
             pltpu.with_memory_space_constraint(mr_steps.reshape(2), pltpu.HBM),
         )
+        sol, res = pl.pallas_call(
+            write_out,
+            out_shape=(out, out),
+            in_specs=[pl.BlockSpec(memory_space=pltpu.VMEM)] * 2,
+            out_specs=(pl.BlockSpec(memory_space=pltpu.HBM),) * 2,
+            scratch_shapes=[pltpu.SemaphoreType.DMA((2,))],
+            compiler_params=pltpu.CompilerParams(vmem_limit_bytes=40 * 2**20),
+        )(sol, res)
         shape = rhs.shape
         return sol.reshape(shape), res.reshape(shape)
 

time: 44 us -> 43.2 us (0.982)
  local copies, waits for them, and re-layouts: 1.24 us -> 0 us
  Pallas kernels: 42 us -> 42.5 us
    unnamed x2 -> x0, local copies, waits for them, and re-layouts: 1.24 us -> none
    pallas_call x0 -> x1, Pallas kernels: none -> 0.65 us  [shards(): pl.pallas_call(write_out, out_shape=(out, out), in_specs=[pl.BlockSpec(me...]
where the time goes in v4:
time: 43.2 us; the launch traced here: 43.1 us
  Pallas kernels  42.5 us (98%)
  between operations  0.64 us (1%)
    pallas_call x1, Pallas kernels, shards(): pl.pallas_call(functools.partial(kernel, time_count, space_count), out_sh...  41.8 us

profile of v4, /device:TPU:16, one launch (start us, length us, event | category | flops | bytes accessed | tf_op | source)
XLA Modules:
  0.0 43.1 jit_solution(13501712112102337124)
XLA Ops:
  0.6 41.8 %shard_map.59 = (f32[2,40,128]{2,1,0:T(8,128)S(1)}, f32[2,40,128]{2,1,0:T(8,128)S(1)}) custom-call(f32[2,40,128]{2,1,0:T(8,128)} %bitcast.12, bf16[4,2,40,40,128]{4,3,2,1,0:T(8,128)(2,1)} %bitcast.10, bf16[2,40,40,128]{3,2,1,0:T(8,128)(2,1)} %bitcast.11, s32[2]{0:T(128)} %bitcast.13), custom_call_target="tpu_custom_call" | custom-call | tf_op jit(solution)/shard_map/pallas_call | solution.py:441
  42.4 0.7 %shard_map.60 = (f32[2,40,128]{2,1,0:T(8,128)}, f32[2,40,128]{2,1,0:T(8,128)}) custom-call(f32[2,40,128]{2,1,0:T(8,128)S(1)} %get-tuple-element.6.sol_in, f32[2,40,128]{2,1,0:T(8,128)S(1)} %get-tuple-element.7.res_in), custom_call_target="tpu_custom_call" | custom-call | tf_op jit(solution)/shard_map/pallas_call | solution.py:480
